TPU v7x, 256 devices: a whole 4x4x8 slice. The times are simulated.
256 devices in a mesh: bank: 8 (over y, x_lo), zero: 32 (over z, x_hi, core).
Axes of the slice: x: 4 (x_hi: 2, x_lo: 2; x = x_hi * 2 + x_lo), y: 4, z: 8, core: 2. Of those that a mesh axis runs over, the one named last changes fastest.
Arguments:
- master_gate: float32 [64, 2048, 1024], P('bank', 'zero'), may hold values from -0.25 to 0.25
- master_up: float32 [64, 2048, 1024], P('bank', 'zero'), may hold values from -0.25 to 0.25
- master_down: float32 [64, 1024, 2048], P('bank', None, 'zero'), may hold values from -0.375 to 0.375
- router_weight: float32 [2048, 64], P('zero', 'bank'), may hold values from -0.125 to 0.125
- router_gain: float32 [2048], P('zero'), may hold values from 0.25 to 1.75
Outputs:
- final_gate: bfloat16 [64, 2048, 1024], P('bank', None, 'zero')
- final_up: bfloat16 [64, 2048, 1024], P('bank', None, 'zero')
- final_down: bfloat16 [64, 1024, 2048], P('bank', 'zero')
- scale_gate: float32 [64, 1024], P('bank', 'zero')
- scale_up: float32 [64, 1024], P('bank', 'zero')
- scale_down: float32 [64, 1024], P('bank', 'zero')
- serve_router: bfloat16 [2048, 64], replicated
All inputs are finite; a program needn't handle non-finite values.
Results may differ from a plain program's by a relative error of at most 0.0085.
Values may be sent and summed in bfloat16 or wider, within the bound.
A program may use at most 64 MiB of HBM per device.

v0:
```python
import jax
import jax.numpy as jnp
from jax import lax
from jax.sharding import PartitionSpec as P


def from_everyone(value, axis):
    copies = jnp.broadcast_to(value, (lax.axis_size(axis), *value.shape))
    return lax.all_to_all(copies, axis, split_axis=0, concat_axis=0, tiled=True)


def over_copies(value, axis):
    everything = from_everyone(value, axis)
    return jnp.sum(everything.astype(jnp.float32), axis=0)


def sent_together(arrays, axis, split_dim, concat_dim, along):
    both = jnp.concatenate(arrays, axis=along)
    whole, at, gathered = (
        lax.all_to_all(both, axis, split_axis=split_dim, concat_axis=concat_dim, tiled=True),
        0,
        [],
    )
    for a in arrays:
        gathered.append(lax.slice_in_dim(whole, at, at + a.shape[along], axis=along))
        at += a.shape[along]
    return tuple(gathered)


def laid_out(tiles, dim):
    lengths = list(tiles.shape[1:])
    lengths[dim] *= tiles.shape[0]
    return jnp.moveaxis(tiles, 0, dim).reshape(lengths)


def gathered_copies(value, axis, dim):
    tiles = from_everyone(value, axis)
    return laid_out(tiles, dim)


def local(master_gate, master_up, master_down, router_weight, router_gain):
    total_gate, total_up, total_down = (
        over_copies(jnp.sum(master_gate * master_gate, axis=1).astype(jnp.bfloat16), "zero").astype(
            jnp.float32
        ),
        over_copies(jnp.sum(master_up * master_up, axis=1).astype(jnp.bfloat16), "zero").astype(
            jnp.float32
        ),
        over_copies(jnp.sum(master_down * master_down, axis=2).astype(jnp.bfloat16), "zero").astype(
            jnp.float32
        ),
    )
    scale_gate = jnp.sqrt(total_gate)
    scale_up = jnp.sqrt(total_up)
    scale_down = jnp.sqrt(total_down)
    narrow_gate, narrow_up, narrow_down = (
        (master_gate / jnp.expand_dims(scale_gate, 1)).astype(jnp.bfloat16),
        (master_up / jnp.expand_dims(scale_up, 1)).astype(jnp.bfloat16),
        (master_down / jnp.expand_dims(scale_down, 2)).astype(jnp.bfloat16),
    )
    final_gate, final_up = sent_together((narrow_gate, narrow_up), "zero", 2, 1, 0)
    final_down = lax.all_to_all(narrow_down, "zero", split_axis=1, concat_axis=2, tiled=True)
    scale_gate = lax.dynamic_slice_in_dim(
        scale_gate, lax.axis_index("zero") * final_gate.shape[2], final_gate.shape[2], axis=1
    )
    scale_up = lax.dynamic_slice_in_dim(
        scale_up, lax.axis_index("zero") * final_up.shape[2], final_up.shape[2], axis=1
    )
    scale_down = lax.dynamic_slice_in_dim(
        scale_down, lax.axis_index("zero") * final_down.shape[1], final_down.shape[1], axis=1
    )
    part_router = (router_weight * router_gain[:, None]).astype(jnp.bfloat16)
    row_router = gathered_copies(part_router, "zero", 0)
    serve_router = gathered_copies(row_router, "bank", 1)
    return (final_gate, final_up, final_down, scale_gate, scale_up, scale_down, serve_router)


def solution(mesh):
    in_specs = (
        P("bank", "zero", None),
        P("bank", "zero", None),
        P("bank", None, "zero"),
        P("zero", "bank"),
        P("zero"),
    )
    out_specs = (
        P("bank", None, "zero"),
        P("bank", None, "zero"),
        P("bank", "zero", None),
        P("bank", "zero"),
        P("bank", "zero"),
        P("bank", "zero"),
        P(),
    )
    return jax.shard_map(local, mesh=mesh, in_specs=in_specs, out_specs=out_specs, check_vma=False)
```

profile of v0, /device:TPU:1, one launch (start us, length us, event | category | flops | bytes accessed | tf_op | source)
XLA Modules:
  0.0 214.5 jit_solution(11568245509490080332)
XLA Ops:
  0.6 0.7 multiply_convert_fusion
  1.3 0.1 reshape.38
  1.5 22.0 %all_to_all.58 = bf16[32,2,256]{2,1,0:T(2,128)(2,1)S(1)} all-to-all(bf16[32,2,256]{2,1,0:T(2,128)(2,1)S(1)} %reshape.38), channel_id=1, replica_groups=mesh['bank'=8,'zero'=32] {'zero'}, dimensions={0} | all-to-all | bytes 65536 | tf_op jit(solution)/shard_map/all_to_all | solution.py:9
  23.5 0.1 reshape.39
  23.6 0.1 reshape.32
  23.7 0.7 broadcast_in_dim.23
  24.4 0.0 copy-start.2
  24.4 4.4 %all-to-all-start.6 = ((bf16[8,2048,8]{1,2,0:T(8,128)(2,1)}), bf16[8,2048,8]{1,2,0:T(8,128)(2,1)S(1)}, u32[]{:S(2)}, u32[]{:S(2)}) async-start(bf16[8,2048,8]{1,2,0:T(8,128)(2,1)} %broadcast_in_dim.23), calls=%async_computation.6 | async-start | bytes 524288 | tf_op jit(solution)/shard_map/all_to_all | solution.py:9
  28.8 1.9 multiply_reduce_fusion
  30.7 4.8 %all-to-all-done.6 = bf16[8,2048,8]{1,2,0:T(8,128)(2,1)S(1)} async-done(((bf16[8,2048,8]{1,2,0:T(8,128)(2,1)}), bf16[8,2048,8]{1,2,0:T(8,128)(2,1)S(1)}, u32[]{:S(2)}, u32[]{:S(2)}) %all-to-all-start.6) | async-done | bytes 262176 | tf_op jit(solution)/shard_map/all_to_all | solution.py:9
  35.5 0.9 broadcast_in_dim.21
  36.4 5.1 %all-to-all-start.3 = ((bf16[32,8,1024]{2,1,0:T(8,128)(2,1)}), bf16[32,8,1024]{2,1,0:T(8,128)(2,1)S(1)}, u32[]{:S(2)}, u32[]{:S(2)}) async-start(bf16[32,8,1024]{2,1,0:T(8,128)(2,1)} %broadcast_in_dim.21), calls=%async_computation.3 | async-start | bytes 1048576 | tf_op jit(solution)/shard_map/all_to_all | solution.py:9
  41.4 0.0 copy-done.2
  41.4 0.3 multiply_reduce_fusion.1
  41.7 17.0 %all-to-all-done.3 = bf16[32,8,1024]{2,1,0:T(8,128)(2,1)S(1)} async-done(((bf16[32,8,1024]{2,1,0:T(8,128)(2,1)}), bf16[32,8,1024]{2,1,0:T(8,128)(2,1)S(1)}, u32[]{:S(2)}, u32[]{:S(2)}) %all-to-all-start.3) | async-done | bytes 524320 | tf_op jit(solution)/shard_map/all_to_all | solution.py:9
  58.7 0.9 broadcast_in_dim.20
  59.6 5.5 %all-to-all-start.1 = ((bf16[32,8,1024]{2,1,0:T(8,128)(2,1)}), bf16[32,8,1024]{2,1,0:T(8,128)(2,1)S(1)}, u32[]{:S(2)}, u32[]{:S(2)}) async-start(bf16[32,8,1024]{2,1,0:T(8,128)(2,1)} %broadcast_in_dim.20), calls=%async_computation.1 | async-start | bytes 1048576 | tf_op jit(solution)/shard_map/all_to_all | solution.py:9
  65.1 0.0 copy-start
  65.1 2.0 multiply_reduce_fusion.2
  67.1 14.8 %all-to-all-done.1 = bf16[32,8,1024]{2,1,0:T(8,128)(2,1)S(1)} async-done(((bf16[32,8,1024]{2,1,0:T(8,128)(2,1)}), bf16[32,8,1024]{2,1,0:T(8,128)(2,1)S(1)}, u32[]{:S(2)}, u32[]{:S(2)}) %all-to-all-start.1) | async-done | bytes 524320 | tf_op jit(solution)/shard_map/all_to_all | solution.py:9
  81.9 0.0 copy-start.3
  81.9 0.9 broadcast_in_dim.19
  82.8 5.9 %all-to-all-start = ((bf16[32,8,1024]{2,1,0:T(8,128)(2,1)}), bf16[32,8,1024]{2,1,0:T(8,128)(2,1)}, u32[]{:S(2)}, u32[]{:S(2)}) async-start(bf16[32,8,1024]{2,1,0:T(8,128)(2,1)} %broadcast_in_dim.19), calls=%async_computation | async-start | bytes 1048576 | tf_op jit(solution)/shard_map/all_to_all | solution.py:9
  88.7 0.0 copy-done
  88.7 2.7 %copy.54 = f32[8,1024,64]{2,0,1:T(8,128)} copy(f32[8,1024,64]{1,2,0:T(8,128)S(1)} %copy-done) | data formatting | bytes 4194304 | tf_op args[2]
  91.5 0.0 copy-done.3
  91.5 0.1 convert_reduce_fusion
  91.6 0.2 copy.53
  91.8 3.9 %fusion.2 = bf16[1024,8,64]{2,1,0:T(8,128)(2,1)} fusion(f32[8,1024,64]{2,0,1:T(8,128)} %copy.54, f32[8,1024]{0,1:T(8,128)S(1)} %copy.53), kind=kLoop, calls=%fused_computation.16 | loop fusion | flops 1048576 | bytes 3178496
  95.6 0.0 copy-start.1
  95.6 4.8 %reshape.36 = bf16[32,2,8192]{2,1,0:T(2,128)(2,1)} reshape(bf16[1024,8,64]{2,1,0:T(8,128)(2,1)} %fusion.2) | data formatting | bytes 2097152
  100.4 5.2 %all-to-all-done = bf16[32,8,1024]{2,1,0:T(8,128)(2,1)} async-done(((bf16[32,8,1024]{2,1,0:T(8,128)(2,1)}), bf16[32,8,1024]{2,1,0:T(8,128)(2,1)}, u32[]{:S(2)}, u32[]{:S(2)}) %all-to-all-start) | async-done | bytes 524320 | tf_op jit(solution)/shard_map/all_to_all | solution.py:9
  105.6 5.8 %all-to-all-start.4 = ((bf16[32,2,8192]{2,1,0:T(2,128)(2,1)}), bf16[32,2,8192]{2,1,0:T(2,128)(2,1)S(1)}, u32[]{:S(2)}, u32[]{:S(2)}) async-start(bf16[32,2,8192]{2,1,0:T(2,128)(2,1)} %reshape.36), calls=%async_computation.4 | async-start | bytes 2097152 | tf_op jit(solution)/shard_map/all_to_all | solution.py:62
  111.4 0.0 copy-done.1
  111.4 2.8 %copy.47 = f32[8,64,1024]{1,0,2:T(8,128)} copy(f32[8,64,1024]{2,1,0:T(8,128)S(1)} %copy-done.1) | data formatting | bytes 4194304 | tf_op args[0]
  114.2 0.0 copy-start.4
  114.2 3.9 %copy.49 = f32[8,64,1024]{1,0,2:T(8,128)} copy(f32[8,64,1024]{2,1,0:T(8,128)} %param.6) | data formatting | bytes 4194304 | tf_op args[1]
  118.1 0.0 copy-done.4
  118.1 0.1 convert_reduce_fusion.1
  118.2 1.1 convert_reduce_fusion.2
  119.3 0.2 copy.46
  119.5 0.2 copy.48
  119.8 6.2 %divide_convert_fusion.1 = (bf16[8,64,1024]{1,0,2:T(8,128)(2,1)S(1)}, bf16[8,64,1024]{1,0,2:T(8,128)(2,1)S(1)}) fusion(f32[8,64,1024]{1,0,2:T(8,128)} %copy.49, f32[8,1024]{0,1:T(8,128)S(1)} %copy.48, f32[8,64,1024]{1,0,2:T(8,128)} %copy.47, f32[8,1024]{0,1:T(8,128)S(1)} %copy.46), kind=kLoop, calls=%fused_computation.2 | loop fusion | flops 2097152 | bytes 6356992 | tf_op jit(solution)/shard_map/convert_element_type | solution.py:58
  126.0 2.9 %fusion.1 = bf16[1024,16,64]{2,1,0:T(8,128)(2,1)} fusion(bf16[8,64,1024]{1,0,2:T(8,128)(2,1)S(1)} %get-tuple-element.9, bf16[8,64,1024]{1,0,2:T(8,128)(2,1)S(1)} %get-tuple-element.10), kind=kLoop, calls=%fused_computation.15 | loop fusion | flops 4194304 | bytes 4194304
  128.8 7.9 %reshape.34 = bf16[32,2,16384]{2,1,0:T(2,128)(2,1)} reshape(bf16[1024,16,64]{2,1,0:T(8,128)(2,1)} %fusion.1) | data formatting | bytes 4194304
  136.7 2.8 %all-to-all-done.4 = bf16[32,2,8192]{2,1,0:T(2,128)(2,1)S(1)} async-done(((bf16[32,2,8192]{2,1,0:T(2,128)(2,1)}), bf16[32,2,8192]{2,1,0:T(2,128)(2,1)S(1)}, u32[]{:S(2)}, u32[]{:S(2)}) %all-to-all-start.4) | async-done | bytes 1048608 | tf_op jit(solution)/shard_map/all_to_all | solution.py:62
  139.5 7.0 %all-to-all-start.2 = ((bf16[32,2,16384]{2,1,0:T(2,128)(2,1)}), bf16[32,2,16384]{2,1,0:T(2,128)(2,1)S(1)}, u32[]{:S(2)}, u32[]{:S(2)}) async-start(bf16[32,2,16384]{2,1,0:T(2,128)(2,1)} %reshape.34), calls=%async_computation.2 | async-start | bytes 4194304 | tf_op jit(solution)/shard_map/all_to_all | solution.py:20
  146.5 0.7 constant_dynamic-slice_fusion
  147.2 0.7 constant_dynamic-slice_fusion.1
  147.8 0.7 constant_dynamic-slice_fusion.2
  148.5 2.4 %reshape.37 = bf16[1024,8,64]{2,1,0:T(8,128)(2,1)} reshape(bf16[32,2,8192]{2,1,0:T(2,128)(2,1)S(1)} %all-to-all-done.4) | data formatting | bytes 2097152
  150.8 4.2 %copy.56 = bf16[8,32,32,64]{3,2,1,0:T(8,128)(2,1)} copy(bf16[8,32,32,64]{3,0,1,2:T(8,128)(2,1)} %bitcast.32) | data formatting | bytes 2097152 | tf_op jit(solution)/shard_map/all_to_all | solution.py:62
  155.1 4.2 %all_to_all.48 = bf16[8,32,2048]{2,1,0:T(8,128)(2,1)} reshape(bf16[8,32,32,64]{3,2,1,0:T(8,128)(2,1)} %copy.56) | data formatting | bytes 2097152 | tf_op jit(solution)/shard_map/all_to_all | solution.py:62
  159.3 37.1 %all-to-all-done.2 = bf16[32,2,16384]{2,1,0:T(2,128)(2,1)S(1)} async-done(((bf16[32,2,16384]{2,1,0:T(2,128)(2,1)}), bf16[32,2,16384]{2,1,0:T(2,128)(2,1)S(1)}, u32[]{:S(2)}, u32[]{:S(2)}) %all-to-all-start.2) | async-done | bytes 2097184 | tf_op jit(solution)/shard_map/all_to_all | solution.py:20
  196.4 4.0 %reshape.35 = bf16[1024,16,64]{2,1,0:T(8,128)(2,1)} reshape(bf16[32,2,16384]{2,1,0:T(2,128)(2,1)S(1)} %all-to-all-done.2) | data formatting | bytes 4194304
  200.4 3.3 %copy.50 = bf16[16,64,1024]{1,2,0:T(8,128)(2,1)S(1)} copy(bf16[16,64,1024]{1,0,2:T(8,128)(2,1)} %bitcast.31) | data formatting | bytes 4194304 | tf_op jit(solution)/shard_map/all_to_all | solution.py:20
  203.6 2.1 fusion
  205.7 0.8 copy.51
  206.5 2.4 %slice.13 = bf16[8,2048,32]{1,2,0:T(8,128)(2,1)} reshape(bf16[8,32,64,32]{2,1,3,0:T(8,128)(2,1)S(1)} %copy.51) | data formatting | bytes 2097152 | tf_op jit(solution)/shard_map/slice | solution.py:25
  209.0 2.4 %copy.52 = bf16[8,32,64,32]{2,1,3,0:T(8,128)(2,1)S(1)} copy(bf16[8,32,64,32]{2,3,1,0:T(8,128)(2,1)} %get-tuple-element.7) | data formatting | bytes 2097152 | tf_op jit(solution)/shard_map/slice | solution.py:25
  211.4 2.4 %slice.15 = bf16[8,2048,32]{1,2,0:T(8,128)(2,1)} reshape(bf16[8,32,64,32]{2,1,3,0:T(8,128)(2,1)S(1)} %copy.52) | data formatting | bytes 2097152 | tf_op jit(solution)/shard_map/slice | solution.py:25
  213.8 0.7 copy.60
  (5 shorter events, 0.1 us)
Async XLA Ops:
  24.4 17.0 %copy-start.2 = (f32[8,64,1024]{2,1,0:T(8,128)S(1)}, f32[8,64,1024]{2,1,0:T(8,128)}, u32[]{:S(2)}) copy-start(f32[8,64,1024]{2,1,0:T(8,128)} %param.6) | copy-start | bytes 6291460
  24.4 11.0 %all-to-all-start.6 = ((bf16[8,2048,8]{1,2,0:T(8,128)(2,1)}), bf16[8,2048,8]{1,2,0:T(8,128)(2,1)S(1)}, u32[]{:S(2)}, u32[]{:S(2)}) async-start(bf16[8,2048,8]{1,2,0:T(8,128)(2,1)} %broadcast_in_dim.23), calls=%async_computation.6 | async-start | bytes 524288 | tf_op jit(solution)/shard_map/all_to_all | solution.py:9
  36.4 22.4 %all-to-all-start.3 = ((bf16[32,8,1024]{2,1,0:T(8,128)(2,1)}), bf16[32,8,1024]{2,1,0:T(8,128)(2,1)S(1)}, u32[]{:S(2)}, u32[]{:S(2)}) async-start(bf16[32,8,1024]{2,1,0:T(8,128)(2,1)} %broadcast_in_dim.21), calls=%async_computation.3 | async-start | bytes 1048576 | tf_op jit(solution)/shard_map/all_to_all | solution.py:9
  59.6 22.3 %all-to-all-start.1 = ((bf16[32,8,1024]{2,1,0:T(8,128)(2,1)}), bf16[32,8,1024]{2,1,0:T(8,128)(2,1)S(1)}, u32[]{:S(2)}, u32[]{:S(2)}) async-start(bf16[32,8,1024]{2,1,0:T(8,128)(2,1)} %broadcast_in_dim.20), calls=%async_computation.1 | async-start | bytes 1048576 | tf_op jit(solution)/shard_map/all_to_all | solution.py:9
  65.1 23.6 %copy-start = (f32[8,1024,64]{1,2,0:T(8,128)S(1)}, f32[8,1024,64]{1,2,0:T(8,128)}, u32[]{:S(2)}) copy-start(f32[8,1024,64]{1,2,0:T(8,128)} %param.7) | copy-start | bytes 6291460
  81.9 9.5 %copy-start.3 = (bf16[32,8,1024]{2,1,0:T(8,128)(2,1)}, bf16[32,8,1024]{2,1,0:T(8,128)(2,1)S(1)}, u32[]{:S(2)}) copy-start(bf16[32,8,1024]{2,1,0:T(8,128)(2,1)S(1)} %all-to-all-done.1) | copy-start | bytes 1572868
  82.8 22.8 %all-to-all-start = ((bf16[32,8,1024]{2,1,0:T(8,128)(2,1)}), bf16[32,8,1024]{2,1,0:T(8,128)(2,1)}, u32[]{:S(2)}, u32[]{:S(2)}) async-start(bf16[32,8,1024]{2,1,0:T(8,128)(2,1)} %broadcast_in_dim.19), calls=%async_computation | async-start | bytes 1048576 | tf_op jit(solution)/shard_map/all_to_all | solution.py:9
  95.6 15.8 %copy-start.1 = (f32[8,64,1024]{2,1,0:T(8,128)S(1)}, f32[8,64,1024]{2,1,0:T(8,128)}, u32[]{:S(2)}) copy-start(f32[8,64,1024]{2,1,0:T(8,128)} %param.5) | copy-start | bytes 6291460
  105.6 33.9 %all-to-all-start.4 = ((bf16[32,2,8192]{2,1,0:T(2,128)(2,1)}), bf16[32,2,8192]{2,1,0:T(2,128)(2,1)S(1)}, u32[]{:S(2)}, u32[]{:S(2)}) async-start(bf16[32,2,8192]{2,1,0:T(2,128)(2,1)} %reshape.36), calls=%async_computation.4 | async-start | bytes 2097152 | tf_op jit(solution)/shard_map/all_to_all | solution.py:62
  114.2 3.9 %copy-start.4 = (bf16[32,8,1024]{2,1,0:T(8,128)(2,1)S(1)}, bf16[32,8,1024]{2,1,0:T(8,128)(2,1)}, u32[]{:S(2)}) copy-start(bf16[32,8,1024]{2,1,0:T(8,128)(2,1)} %copy-done.3) | copy-start | bytes 1572868
  139.5 56.9 %all-to-all-start.2 = ((bf16[32,2,16384]{2,1,0:T(2,128)(2,1)}), bf16[32,2,16384]{2,1,0:T(2,128)(2,1)S(1)}, u32[]{:S(2)}, u32[]{:S(2)}) async-start(bf16[32,2,16384]{2,1,0:T(2,128)(2,1)} %reshape.34), calls=%async_computation.2 | async-start | bytes 4194304 | tf_op jit(solution)/shard_map/all_to_all | solution.py:20
where the time goes:
time: 216 us; the launch traced here: 214 us
  waiting for transfers between devices  81.7 us (38%)
  local copies, waits for them, and re-layouts  57.3 us (27%)
  starting transfers between devices  33.5 us (16%)
  blocking collectives  22 us (10%)
  other arithmetic  19.1 us (9%)
    all_to_all x4, waiting for transfers between devices, from_everyone(): return lax.all_to_all(copies, axis, split_axis=0, concat_axis=0, tiled=True)  41.8 us
    all_to_all x1, waiting for transfers between devices, sent_together(): lax.all_to_all(both, axis, split_axis=split_dim, concat_axis=concat_dim,...  37.1 us
    unnamed x21, local copies, waits for them, and re-layouts  29.3 us
    all_to_all x1, blocking collectives, from_everyone(): return lax.all_to_all(copies, axis, split_axis=0, concat_axis=0, tiled=True)  22 us
    all_to_all x4, starting transfers between devices, from_everyone(): return lax.all_to_all(copies, axis, split_axis=0, concat_axis=0, tiled=True)  20.8 us
    slice x5, local copies, waits for them, and re-layouts, sent_together(): lax.slice_in_dim(whole, at, at + a.shape[along], axis=along)  10.1 us
    all_to_all x2, local copies, waits for them, and re-layouts, local(): lax.all_to_all(narrow_down, 'zero', split_axis=1, concat_axis=2, tiled=True)  8.47 us
    all_to_all x1, starting transfers between devices, sent_together(): lax.all_to_all(both, axis, split_axis=split_dim, concat_axis=concat_dim,...  6.96 us
  transfers between devices with their start and end apart: 6, of which 6 were waited for; matrix products, arithmetic and copies ran while one was open for 23% of the time, Pallas kernels for 0%

commit v1 on v0

--- a/solution.py
+++ b/solution.py
@@ -59,7 +59,12 @@
         (master_down / jnp.expand_dims(scale_down, 2)).astype(jnp.bfloat16),
     )
     final_gate, final_up = sent_together((narrow_gate, narrow_up), "zero", 2, 1, 0)
-    final_down = lax.all_to_all(narrow_down, "zero", split_axis=1, concat_axis=2, tiled=True)
+    final_down = jnp.concatenate(
+        lax.all_to_all(
+            jnp.stack(jnp.split(narrow_down, lax.axis_size("zero"), axis=1), axis=0), "zero", 0, 0
+        ),
+        axis=2,
+    )
     scale_gate = lax.dynamic_slice_in_dim(
         scale_gate, lax.axis_index("zero") * final_gate.shape[2], final_gate.shape[2], axis=1
     )

time: 216 us -> 226 us (1.046)
  blocking collectives: 22 us -> 0 us
  local copies, waits for them, and re-layouts: 57.3 us -> 78.7 us
  starting transfers between devices: 33.5 us -> 44.7 us
    all_to_all x1 -> x0, blocking collectives: 22 us -> none  [from_everyone(): return lax.all_to_all(copies, axis, split_axis=0, concat_axis=0, tiled=True)]
    unnamed x21 -> x56, local copies, waits for them, and re-layouts: 29.3 us -> 50.3 us
    all_to_all x4 -> x5, starting transfers between devices: 20.8 us -> 32.9 us  [from_everyone(): return lax.all_to_all(copies, axis, split_axis=0, concat_axis=0, tiled=True)]
    all_to_all x2 -> x0, local copies, waits for them, and re-layouts: 8.47 us -> none  [local(): lax.all_to_all(narrow_down, 'zero', split_axis=1, concat_axis=2, tiled=True)]
    reshape x0 -> x2, local copies, waits for them, and re-layouts: none -> 8.47 us  [local(): jnp.concatenate(lax.all_to_all(jnp.stack(jnp.split(narrow_down, lax.axis_...]
    unnamed x2 -> x1, other arithmetic: 6.73 us -> 2.88 us
    convert_element_type x0 -> x1, other arithmetic: none -> 2.88 us  [local(): (master_down / jnp.expand_dims(scale_down, 2)).astype(jnp.bfloat16)]
    all_to_all x4 -> x5, waiting for transfers between devices: 41.8 us -> 42.3 us  [from_everyone(): return lax.all_to_all(copies, axis, split_axis=0, concat_axis=0, tiled=True)]
  transfers between devices with their start and end apart: 6 -> 7, of which waited for: 6 -> 6; matrix products, arithmetic and copies ran while one was open for 23% -> 32% of each run, Pallas kernels for 0% -> 0%
where the time goes in v1:
time: 226 us; the launch traced here: 225 us
  waiting for transfers between devices  83.1 us (37%)
  local copies, waits for them, and re-layouts  78.7 us (35%)
  starting transfers between devices  44.7 us (20%)
  other arithmetic  17.2 us (8%)
    unnamed x56, local copies, waits for them, and re-layouts  50.3 us
    all_to_all x5, waiting for transfers between devices, from_everyone(): return lax.all_to_all(copies, axis, split_axis=0, concat_axis=0, tiled=True)  42.3 us
    all_to_all x1, waiting for transfers between devices, sent_together(): lax.all_to_all(both, axis, split_axis=split_dim, concat_axis=concat_dim,...  37.1 us
    all_to_all x5, starting transfers between devices, from_everyone(): return lax.all_to_all(copies, axis, split_axis=0, concat_axis=0, tiled=True)  32.9 us
    slice x5, local copies, waits for them, and re-layouts, sent_together(): lax.slice_in_dim(whole, at, at + a.shape[along], axis=along)  10.1 us
    reshape x2, local copies, waits for them, and re-layouts, local(): jnp.concatenate(lax.all_to_all(jnp.stack(jnp.split(narrow_down, lax.axis_...  8.47 us
    convert_element_type x1, other arithmetic, local(): (master_up / jnp.expand_dims(scale_up, 1)).astype(jnp.bfloat16)  6.19 us
    all_to_all x1, starting transfers between devices, sent_together(): lax.all_to_all(both, axis, split_axis=split_dim, concat_axis=concat_dim,...  5.97 us
  transfers between devices with their start and end apart: 7, of which 6 were waited for; matrix products, arithmetic and copies ran while one was open for 32% of the time, Pallas kernels for 0%

profile of v1, /device:TPU:1, one launch (start us, length us, event | category | flops | bytes accessed | tf_op | source)
XLA Modules:
  0.0 224.6 jit_solution(9869695012994616359)
XLA Ops:
  0.6 0.8 multiply_convert_fusion
  1.5 0.7 reshape.46
  2.2 12.6 %all-to-all-start.5 = ((bf16[32,2,256]{2,1,0:T(2,128)(2,1)}), bf16[32,2,256]{2,1,0:T(2,128)(2,1)S(1)}, u32[]{:S(2)}, u32[]{:S(2)}) async-start(bf16[32,2,256]{2,1,0:T(2,128)(2,1)} %reshape.46), calls=%async_computation.5 | async-start | bytes 65536 | tf_op jit(solution)/shard_map/all_to_all | solution.py:9
  14.8 1.9 multiply_reduce_fusion
  16.7 7.8 %all-to-all-done.5 = bf16[32,2,256]{2,1,0:T(2,128)(2,1)S(1)} async-done(((bf16[32,2,256]{2,1,0:T(2,128)(2,1)}), bf16[32,2,256]{2,1,0:T(2,128)(2,1)S(1)}, u32[]{:S(2)}, u32[]{:S(2)}) %all-to-all-start.5) | async-done | bytes 32800 | tf_op jit(solution)/shard_map/all_to_all | solution.py:9
  24.4 0.9 broadcast_in_dim.21
  25.3 3.9 %all-to-all-start.3 = ((bf16[32,8,1024]{2,1,0:T(8,128)(2,1)}), bf16[32,8,1024]{2,1,0:T(8,128)(2,1)S(1)}, u32[]{:S(2)}, u32[]{:S(2)}) async-start(bf16[32,8,1024]{2,1,0:T(8,128)(2,1)} %broadcast_in_dim.21), calls=%async_computation.3 | async-start | bytes 1048576 | tf_op jit(solution)/shard_map/all_to_all | solution.py:9
  29.3 2.7 %copy.47 = f32[8,1024,64]{2,1,0:T(8,128)} copy(f32[8,1024,64]{1,2,0:T(8,128)S(1)} %copy-done) | data formatting | bytes 4194304 | tf_op args[2]
  32.0 2.0 multiply_reduce_fusion.1
  34.7 11.8 %all-to-all-done.3 = bf16[32,8,1024]{2,1,0:T(8,128)(2,1)S(1)} async-done(((bf16[32,8,1024]{2,1,0:T(8,128)(2,1)}), bf16[32,8,1024]{2,1,0:T(8,128)(2,1)S(1)}, u32[]{:S(2)}, u32[]{:S(2)}) %all-to-all-start.3) | async-done | bytes 524320 | tf_op jit(solution)/shard_map/all_to_all | solution.py:9
  46.5 0.7 broadcast_in_dim.23
  47.3 4.2 %all-to-all-start.6 = ((bf16[8,2048,8]{1,2,0:T(8,128)(2,1)}), bf16[8,2048,8]{1,2,0:T(8,128)(2,1)S(1)}, u32[]{:S(2)}, u32[]{:S(2)}) async-start(bf16[8,2048,8]{1,2,0:T(8,128)(2,1)} %broadcast_in_dim.23), calls=%async_computation.6 | async-start | bytes 524288 | tf_op jit(solution)/shard_map/all_to_all | solution.py:9
  51.6 2.9 %divide_convert_fusion = bf16[8,1024,64]{2,1,0:T(8,128)(2,1)S(1)} fusion(f32[8,1024,64]{2,1,0:T(8,128)} %copy.47, f32[8,1024]{1,0:T(8,128)S(1)} %sqrt.23), kind=kLoop, calls=%fused_computation.1 | loop fusion | flops 1048576 | bytes 3178496 | tf_op jit(solution)/shard_map/convert_element_type | solution.py:59
  55.1 0.6 constant_dynamic-update-slice_fusion.30
  55.7 0.6 constant_dynamic-update-slice_fusion.29
  56.3 0.6 constant_dynamic-update-slice_fusion.28
  57.0 0.6 constant_dynamic-update-slice_fusion.27
  58.9 0.6 constant_dynamic-update-slice_fusion.24
  60.1 0.6 constant_dynamic-update-slice_fusion.22
  62.0 0.6 constant_dynamic-update-slice_fusion.19
  62.6 0.6 constant_dynamic-update-slice_fusion.18
  63.8 0.6 constant_dynamic-update-slice_fusion.16
  64.5 0.6 constant_dynamic-update-slice_fusion.15
  65.1 0.6 constant_dynamic-update-slice_fusion.14
  65.7 0.6 constant_dynamic-update-slice_fusion.13
  67.0 0.6 constant_dynamic-update-slice_fusion.11
  67.6 0.6 constant_dynamic-update-slice_fusion.10
  68.2 0.9 broadcast_in_dim.20
  69.1 6.4 %all-to-all-start.1 = ((bf16[32,8,1024]{2,1,0:T(8,128)(2,1)}), bf16[32,8,1024]{2,1,0:T(8,128)(2,1)S(1)}, u32[]{:S(2)}, u32[]{:S(2)}) async-start(bf16[32,8,1024]{2,1,0:T(8,128)(2,1)} %broadcast_in_dim.20), calls=%async_computation.1 | async-start | bytes 1048576 | tf_op jit(solution)/shard_map/all_to_all | solution.py:9
  75.5 0.6 constant_dynamic-update-slice_fusion.9
  76.7 0.6 constant_dynamic-update-slice_fusion.7
  77.3 0.6 constant_dynamic-update-slice_fusion.6
  77.9 0.6 constant_dynamic-update-slice_fusion.5
  78.6 13.7 %all-to-all-done.1 = bf16[32,8,1024]{2,1,0:T(8,128)(2,1)S(1)} async-done(((bf16[32,8,1024]{2,1,0:T(8,128)(2,1)}), bf16[32,8,1024]{2,1,0:T(8,128)(2,1)S(1)}, u32[]{:S(2)}, u32[]{:S(2)}) %all-to-all-start.1) | async-done | bytes 524320 | tf_op jit(solution)/shard_map/all_to_all | solution.py:9
  92.3 0.9 broadcast_in_dim.19
  93.2 5.8 %all-to-all-start = ((bf16[32,8,1024]{2,1,0:T(8,128)(2,1)}), bf16[32,8,1024]{2,1,0:T(8,128)(2,1)S(1)}, u32[]{:S(2)}, u32[]{:S(2)}) async-start(bf16[32,8,1024]{2,1,0:T(8,128)(2,1)} %broadcast_in_dim.19), calls=%async_computation | async-start | bytes 1048576 | tf_op jit(solution)/shard_map/all_to_all | solution.py:9
  100.3 0.6 constant_dynamic-update-slice_fusion.2
  101.5 0.6 constant_dynamic-update-slice_fusion
  102.2 4.8 %reshape.44 = bf16[32,2,8192]{2,1,0:T(2,128)(2,1)} reshape(bf16[32,8,32,64]{3,2,1,0:T(8,128)(2,1)} %constant_dynamic-update-slice_fusion) | data formatting | bytes 2097152
  107.0 8.9 %all-to-all-done = bf16[32,8,1024]{2,1,0:T(8,128)(2,1)S(1)} async-done(((bf16[32,8,1024]{2,1,0:T(8,128)(2,1)}), bf16[32,8,1024]{2,1,0:T(8,128)(2,1)S(1)}, u32[]{:S(2)}, u32[]{:S(2)}) %all-to-all-start) | async-done | bytes 524320 | tf_op jit(solution)/shard_map/all_to_all | solution.py:9
  115.9 0.8 copy-done.5
  116.7 5.8 %all-to-all-start.4 = ((bf16[32,2,8192]{2,1,0:T(2,128)(2,1)}), bf16[32,2,8192]{2,1,0:T(2,128)(2,1)S(1)}, u32[]{:S(2)}, u32[]{:S(2)}) async-start(bf16[32,2,8192]{2,1,0:T(2,128)(2,1)} %reshape.44), calls=%async_computation.4 | async-start | bytes 2097152 | tf_op jit(solution)/shard_map/all_to_all | solution.py:63
  122.5 2.7 %copy.43 = f32[8,64,1024]{1,0,2:T(8,128)} copy(f32[8,64,1024]{2,1,0:T(8,128)S(1)} %copy-done.1) | data formatting | bytes 4194304 | tf_op args[1]
  125.3 3.9 %copy.41 = f32[8,64,1024]{1,0,2:T(8,128)} copy(f32[8,64,1024]{2,1,0:T(8,128)} %param.5) | data formatting | bytes 4194304 | tf_op args[0]
  129.8 6.2 %divide_convert_fusion.1 = (bf16[8,64,1024]{1,0,2:T(8,128)(2,1)S(1)}, bf16[8,64,1024]{1,0,2:T(8,128)(2,1)S(1)}) fusion(f32[8,64,1024]{1,0,2:T(8,128)} %copy.43, f32[8,1024]{0,1:T(8,128)S(1)} %copy.42, f32[8,64,1024]{1,0,2:T(8,128)} %copy.41, f32[8,1024]{0,1:T(8,128)S(1)} %copy.40), kind=kLoop, calls=%fused_computation.2 | loop fusion | flops 2097152 | bytes 6356992 | tf_op jit(solution)/shard_map/convert_element_type | solution.py:58
  136.0 2.9 %fusion.1 = bf16[1024,16,64]{2,1,0:T(8,128)(2,1)} fusion(bf16[8,64,1024]{1,0,2:T(8,128)(2,1)S(1)} %get-tuple-element.9, bf16[8,64,1024]{1,0,2:T(8,128)(2,1)S(1)} %get-tuple-element.10), kind=kLoop, calls=%fused_computation.79 | loop fusion | flops 4194304 | bytes 4194304
  138.9 7.9 %reshape.42 = bf16[32,2,16384]{2,1,0:T(2,128)(2,1)} reshape(bf16[1024,16,64]{2,1,0:T(8,128)(2,1)} %fusion.1) | data formatting | bytes 4194304
  146.8 3.8 %all-to-all-done.4 = bf16[32,2,8192]{2,1,0:T(2,128)(2,1)S(1)} async-done(((bf16[32,2,8192]{2,1,0:T(2,128)(2,1)}), bf16[32,2,8192]{2,1,0:T(2,128)(2,1)S(1)}, u32[]{:S(2)}, u32[]{:S(2)}) %all-to-all-start.4) | async-done | bytes 1048608 | tf_op jit(solution)/shard_map/all_to_all | solution.py:63
  150.6 6.0 %all-to-all-start.2 = ((bf16[32,2,16384]{2,1,0:T(2,128)(2,1)}), bf16[32,2,16384]{2,1,0:T(2,128)(2,1)S(1)}, u32[]{:S(2)}, u32[]{:S(2)}) async-start(bf16[32,2,16384]{2,1,0:T(2,128)(2,1)} %reshape.42), calls=%async_computation.2 | async-start | bytes 4194304 | tf_op jit(solution)/shard_map/all_to_all | solution.py:20
  156.6 0.7 constant_dynamic-slice_fusion.2
  157.2 0.7 constant_dynamic-slice_fusion.1
  157.9 0.7 constant_dynamic-slice_fusion
  158.6 2.4 %reshape.45 = bf16[32,8,32,64]{3,2,1,0:T(8,128)(2,1)} reshape(bf16[32,2,8192]{2,1,0:T(2,128)(2,1)S(1)} %all-to-all-done.4) | data formatting | bytes 2097152
  160.9 4.2 %copy.48 = bf16[8,32,32,64]{3,2,1,0:T(8,128)(2,1)} copy(bf16[8,32,32,64]{3,1,0,2:T(8,128)(2,1)} %bitcast.155) | data formatting | bytes 2097152 | tf_op jit(solution)/shard_map/reshape | solution.py:62
  165.2 4.2 %reshape.39 = bf16[8,32,2048]{2,1,0:T(8,128)(2,1)} reshape(bf16[8,32,32,64]{3,2,1,0:T(8,128)(2,1)} %copy.48) | data formatting | bytes 2097152 | tf_op jit(solution)/shard_map/reshape | solution.py:62
  169.4 37.1 %all-to-all-done.2 = bf16[32,2,16384]{2,1,0:T(2,128)(2,1)S(1)} async-done(((bf16[32,2,16384]{2,1,0:T(2,128)(2,1)}), bf16[32,2,16384]{2,1,0:T(2,128)(2,1)S(1)}, u32[]{:S(2)}, u32[]{:S(2)}) %all-to-all-start.2) | async-done | bytes 2097184 | tf_op jit(solution)/shard_map/all_to_all | solution.py:20
  206.5 4.0 %reshape.43 = bf16[1024,16,64]{2,1,0:T(8,128)(2,1)} reshape(bf16[32,2,16384]{2,1,0:T(2,128)(2,1)S(1)} %all-to-all-done.2) | data formatting | bytes 4194304
  210.5 3.3 %copy.44 = bf16[16,64,1024]{1,2,0:T(8,128)(2,1)S(1)} copy(bf16[16,64,1024]{1,0,2:T(8,128)(2,1)} %bitcast.154) | data formatting | bytes 4194304 | tf_op jit(solution)/shard_map/all_to_all | solution.py:20
  213.7 2.1 fusion
  215.8 0.8 copy.45
  216.6 2.4 %slice.13 = bf16[8,2048,32]{1,2,0:T(8,128)(2,1)} reshape(bf16[8,32,64,32]{2,1,3,0:T(8,128)(2,1)S(1)} %copy.45) | data formatting | bytes 2097152 | tf_op jit(solution)/shard_map/slice | solution.py:25
  219.0 2.4 %copy.46 = bf16[8,32,64,32]{2,1,3,0:T(8,128)(2,1)S(1)} copy(bf16[8,32,64,32]{2,3,1,0:T(8,128)(2,1)} %get-tuple-element.7) | data formatting | bytes 2097152 | tf_op jit(solution)/shard_map/slice | solution.py:25
  221.4 2.4 %slice.15 = bf16[8,2048,32]{1,2,0:T(8,128)(2,1)} reshape(bf16[8,32,64,32]{2,1,3,0:T(8,128)(2,1)S(1)} %copy.46) | data formatting | bytes 2097152 | tf_op jit(solution)/shard_map/slice | solution.py:25
  223.9 0.7 copy.82
  (39 shorter events, 8.9 us)
Async XLA Ops:
  0.6 28.6 %copy-start = (f32[8,1024,64]{1,2,0:T(8,128)S(1)}, f32[8,1024,64]{1,2,0:T(8,128)}, u32[]{:S(2)}) copy-start(f32[8,1024,64]{1,2,0:T(8,128)} %param.7) | copy-start | bytes 6291460
  2.2 22.2 %all-to-all-start.5 = ((bf16[32,2,256]{2,1,0:T(2,128)(2,1)}), bf16[32,2,256]{2,1,0:T(2,128)(2,1)S(1)}, u32[]{:S(2)}, u32[]{:S(2)}) async-start(bf16[32,2,256]{2,1,0:T(2,128)(2,1)} %reshape.46), calls=%async_computation.5 | async-start | bytes 65536 | tf_op jit(solution)/shard_map/all_to_all | solution.py:9
  25.3 21.3 %all-to-all-start.3 = ((bf16[32,8,1024]{2,1,0:T(8,128)(2,1)}), bf16[32,8,1024]{2,1,0:T(8,128)(2,1)S(1)}, u32[]{:S(2)}, u32[]{:S(2)}) async-start(bf16[32,8,1024]{2,1,0:T(8,128)(2,1)} %broadcast_in_dim.21), calls=%async_computation.3 | async-start | bytes 1048576 | tf_op jit(solution)/shard_map/all_to_all | solution.py:9
  32.0 2.2 copy-start.2
  47.3 21.0 %all-to-all-start.6 = ((bf16[8,2048,8]{1,2,0:T(8,128)(2,1)}), bf16[8,2048,8]{1,2,0:T(8,128)(2,1)S(1)}, u32[]{:S(2)}, u32[]{:S(2)}) async-start(bf16[8,2048,8]{1,2,0:T(8,128)(2,1)} %broadcast_in_dim.23), calls=%async_computation.6 | async-start | bytes 524288 | tf_op jit(solution)/shard_map/all_to_all | solution.py:9
  69.1 23.2 %all-to-all-start.1 = ((bf16[32,8,1024]{2,1,0:T(8,128)(2,1)}), bf16[32,8,1024]{2,1,0:T(8,128)(2,1)S(1)}, u32[]{:S(2)}, u32[]{:S(2)}) async-start(bf16[32,8,1024]{2,1,0:T(8,128)(2,1)} %broadcast_in_dim.20), calls=%async_computation.1 | async-start | bytes 1048576 | tf_op jit(solution)/shard_map/all_to_all | solution.py:9
  92.3 14.6 %copy-start.3 = (bf16[32,8,1024]{2,1,0:T(8,128)(2,1)}, bf16[32,8,1024]{2,1,0:T(8,128)(2,1)S(1)}, u32[]{:S(2)}) copy-start(bf16[32,8,1024]{2,1,0:T(8,128)(2,1)S(1)} %all-to-all-done.1) | copy-start | bytes 1572868
  93.2 22.7 %all-to-all-start = ((bf16[32,8,1024]{2,1,0:T(8,128)(2,1)}), bf16[32,8,1024]{2,1,0:T(8,128)(2,1)S(1)}, u32[]{:S(2)}, u32[]{:S(2)}) async-start(bf16[32,8,1024]{2,1,0:T(8,128)(2,1)} %broadcast_in_dim.19), calls=%async_computation | async-start | bytes 1048576 | tf_op jit(solution)/shard_map/all_to_all | solution.py:9
  102.2 20.4 %copy-start.1 = (f32[8,64,1024]{2,1,0:T(8,128)S(1)}, f32[8,64,1024]{2,1,0:T(8,128)}, u32[]{:S(2)}) copy-start(f32[8,64,1024]{2,1,0:T(8,128)} %param.6) | copy-start | bytes 6291460
  115.9 0.8 copy-start.5
  116.7 33.9 %all-to-all-start.4 = ((bf16[32,2,8192]{2,1,0:T(2,128)(2,1)}), bf16[32,2,8192]{2,1,0:T(2,128)(2,1)S(1)}, u32[]{:S(2)}, u32[]{:S(2)}) async-start(bf16[32,2,8192]{2,1,0:T(2,128)(2,1)} %reshape.44), calls=%async_computation.4 | async-start | bytes 2097152 | tf_op jit(solution)/shard_map/all_to_all | solution.py:63
  125.3 4.0 %copy-start.4 = (bf16[32,8,1024]{2,1,0:T(8,128)(2,1)S(1)}, bf16[32,8,1024]{2,1,0:T(8,128)(2,1)}, u32[]{:S(2)}) copy-start(bf16[32,8,1024]{2,1,0:T(8,128)(2,1)} %copy-done.3) | copy-start | bytes 1572868
  125.3 4.3 %copy-start.6 = (bf16[32,8,1024]{2,1,0:T(8,128)(2,1)S(1)}, bf16[32,8,1024]{2,1,0:T(8,128)(2,1)}, u32[]{:S(2)}) copy-start(bf16[32,8,1024]{2,1,0:T(8,128)(2,1)} %copy-done.5) | copy-start | bytes 1572868
  150.6 55.9 %all-to-all-start.2 = ((bf16[32,2,16384]{2,1,0:T(2,128)(2,1)}), bf16[32,2,16384]{2,1,0:T(2,128)(2,1)S(1)}, u32[]{:S(2)}, u32[]{:S(2)}) async-start(bf16[32,2,16384]{2,1,0:T(2,128)(2,1)} %reshape.42), calls=%async_computation.2 | async-start | bytes 4194304 | tf_op jit(solution)/shard_map/all_to_all | solution.py:20
